TPU v7x, 256 devices: a whole 4x4x8 slice. The times are simulated.
256 devices in a mesh: dp: 32 (over y, z), group: 8 (over x, core).
Axes of the slice: x: 4, y: 4, z: 8, core: 2. Of those that a mesh axis runs over, the one named last changes fastest.
Arguments:
- keys: int32 [131072], P(('dp', 'group')), may hold values from 0 to 1073741823
- cut: int32 [1], replicated, may hold values from 256 to 1023
- owner: int32 [131072, 1], P(('dp', 'group')), may hold values from 0 to 31; in each aligned block of 512 rows (0 to 511, 512 to 1023, ...) at most 32 rows name the same one
- tokens: int32 [131072, 2048], P(('dp', 'group')), may hold values from 0 to 128255
Outputs:
- histogram: int32 [4096], replicated
- packed_rows: int32 [262144, 2048], P(('dp', 'group'))
- packed_weights: float32 [262144], P(('dp', 'group'))
Inputs may be any that keep to these rules, and one draw needn't show every extreme that they name: Among the examples of one device, at most 32 have the same owner, and some owner has exactly 32.
All inputs are finite; a program needn't handle non-finite values.
Results may differ from a plain program's by a relative error of at most 0.0003.
Values sent between devices are 32-bit elements; how exact they have to be, the bound alone decides.
A program may use at most 128 MiB of HBM per device.

v0:
```python
import jax
import jax.numpy as jnp
from jax import lax
from jax.sharding import Mesh
from jax.sharding import PartitionSpec as P

BINS = 4096
BIN_WIDTH = 262144
DP = ("dp_0", "dp_1")
GROUP = ("group_0", "group_1")
DP_GROUP = ("dp_0", "dp_1", "group_0", "group_1")


def neutral_like(value, identity):
    return jnp.broadcast_to(jnp.asarray(identity, value.dtype), value.shape)


def prefix_by_axis(value, axes, combine, identity):
    before = start = neutral_like(value, identity)
    so_far = value
    for axis in reversed(axes):
        count, index = (lax.axis_size(axis), lax.axis_index(axis))
        pieces = lax.all_gather(so_far, axis)
        inside, so_far = (start, start)
        for k in range(count):
            passed = k < index
            so_far = combine(so_far, pieces[k])
            inside = jnp.where(passed, so_far, inside)
        before = combine(inside, before)
    return before


def split_up(value, dim, count):
    before, after = (value.shape[:dim], value.shape[dim + 1 :])
    return jnp.moveaxis(value.reshape(*before, count, -1, *after), dim, 0)


def laid_out(tiles, dim):
    tiles = jnp.moveaxis(tiles, 0, dim)
    dims = tiles.shape
    return tiles.reshape(*dims[:dim], dims[dim] * dims[dim + 1], *dims[dim + 2 :])


def exchange_both(value, axis, axes, splits, concats):
    sizes = [lax.axis_size(a) for a in axes]
    tiles = split_up(value, splits[0], sizes[0])
    tiles = jnp.moveaxis(split_up(tiles, splits[1] + 1, sizes[1]), 0, 1)
    inside = tiles.shape[2:]
    tiles = tiles.reshape(-1, *inside)
    tiles = lax.all_to_all(tiles, axis, split_axis=0, concat_axis=0, tiled=True)
    tiles = laid_out(tiles.reshape(*sizes, *inside), concats[0] + 1)
    return laid_out(tiles, concats[1])


def add_counts(earlier, later):
    return earlier + later


def body(keys, cut, owner, tokens):
    examples = keys.shape[0]
    width = tokens.shape[1]
    n_owner = lax.axis_size(DP)
    n_member = lax.axis_size(GROUP)
    slots = 2 * examples // (n_owner * n_member)
    capacity = 2 * examples
    bins_of = keys // BIN_WIDTH
    local_hist = jnp.zeros((BINS,), jnp.float32).at[bins_of].add(1.0)
    kept = bins_of >= cut[0]
    dest = owner[:, 0]
    onehot = (
        (dest[:, None] == jnp.arange(n_owner, dtype=jnp.int32)[None, :]) & kept[:, None]
    ).astype(jnp.int32)
    counts = jnp.sum(onehot, axis=0).astype(jnp.float32)
    before = prefix_by_axis(counts, DP_GROUP, add_counts, jnp.zeros_like(counts))
    hist = lax.psum(local_hist, DP_GROUP)
    running = jnp.cumsum(onehot, axis=0) - onehot
    local_rank = jnp.sum(running * onehot, axis=1)
    offset = jnp.sum(before.astype(jnp.int32)[None, :] * onehot, axis=1)
    rank = offset + local_rank
    member = rank % n_member
    outside = n_owner * n_member * slots
    position_send = jnp.where(
        kept, (dest * n_member + member) * slots + local_rank // n_member, outside
    )
    send_rows = jnp.zeros((outside, width), jnp.int32).at[position_send].set(tokens, mode="drop")
    details = jnp.stack([rank // n_member, keys], axis=1)
    send_meta = jnp.full((outside, 2), -1, jnp.int32).at[position_send].set(details, mode="drop")
    send_rows = send_rows.reshape(n_owner, n_member, slots, width)
    send_meta = send_meta.reshape(n_owner, n_member, slots, 2)
    got_rows, got_meta = (
        exchange_both(send_rows, DP_GROUP, (DP, GROUP), (0, 1), (0, 1)),
        exchange_both(send_meta, DP_GROUP, (DP, GROUP), (0, 1), (0, 1)),
    )
    got_rows = got_rows.reshape(-1, width)
    got_meta = got_meta.reshape(-1, 2)
    slot = got_meta[:, 0]
    valid = slot >= 0
    target = jnp.where(valid, slot, capacity)
    suffix = jnp.cumsum(hist[::-1])[::-1]
    total = jnp.maximum(suffix[cut[0]], 1.0)
    got_bins = jnp.clip(got_meta[:, 1] // BIN_WIDTH, 0, BINS - 1)
    weight = jnp.where(valid, suffix[got_bins] / total, 0.0)
    packed_rows = jnp.zeros((capacity, width), jnp.int32).at[target].set(got_rows, mode="drop")
    packed_weights = jnp.zeros((capacity,), jnp.float32).at[target].set(weight, mode="drop")
    return (hist.astype(jnp.int32), packed_rows, packed_weights)


def solution(mesh):
    torus = Mesh(mesh.devices.reshape(4, 8, 4, 2), ("dp_0", "dp_1", "group_0", "group_1"))
    placed = (P(DP_GROUP), P(), P(DP_GROUP, None), P(DP_GROUP, None))
    return jax.shard_map(
        body,
        mesh=torus,
        in_specs=placed,
        out_specs=(P(), P(DP_GROUP, None), P(DP_GROUP)),
        check_vma=False,
    )
```

profile of v0, /device:TPU:1, one launch (start us, length us, event | category | flops | bytes accessed | tf_op | source)
XLA Modules:
  0.0 360.7 jit_solution(18366167405808590215)
XLA Ops:
  1.3 0.7 broadcast_compare_fusion
  2.0 0.8 convert_reduce_fusion
  2.8 1.3 dynamic-slice
  4.8 5.3 %all-reduce = f32[64]{0:T(128)S(1)} all-reduce(f32[64]{0:T(128)S(1)} %convert_dynamic-update-slice_fusion), channel_id=2, replica_groups=mesh['dp_0'=4,'dp_1'=8,'group_0'=4,'group_1'=2] {'group_1'}, use_global_device_ids=true, to_apply=%add | all-reduce | flops 64 | bytes 512
  10.1 1.3 dynamic-slice.1
  12.2 6.7 %all-reduce.1 = f32[128]{0:T(128)S(1)} all-reduce(f32[128]{0:T(128)S(1)} %fusion.35), channel_id=3, replica_groups=mesh['dp_0'=4,'dp_1'=8,'group_0'=4,'group_1'=2] {'group_0'}, use_global_device_ids=true, to_apply=%add.1 | all-reduce | flops 128 | bytes 1024
  19.0 15.4 %all-gather.2 = f32[8,1,32]{2,1,0:T(1,128)S(1)} all-gather(f32[1,1,32]{2,1,0:T(1,128)S(1)} %fusion.37), channel_id=1, replica_groups=mesh['dp_0'=4,'dp_1'=8,'group_0'=4,'group_1'=2] {'dp_1'}, dimensions={0}, use_global_device_ids=true | all-gather | bytes 1152 | tf_op jit(solution)/shard_map/all_gather | solution.py:23
  34.4 7.9 %all-gather.3 = f32[4,1,32]{2,1,0:T(1,128)S(1)} all-gather(f32[1,1,32]{2,1,0:T(1,128)S(1)} %bitcast.115), channel_id=1, replica_groups=mesh['dp_0'=4,'dp_1'=8,'group_0'=4,'group_1'=2] {'dp_0'}, dimensions={0}, use_global_device_ids=true | all-gather | bytes 640 | tf_op jit(solution)/shard_map/all_gather | solution.py:23
  42.4 0.7 fusion.10
  43.1 1.2 reduce-window.15
  44.6 0.8 select_reduce_fusion
  45.4 0.7 compare_select_fusion.6
  47.0 1.8 scatter_custom_fusion.1
  48.8 2.3 copy.14
  51.1 13.2 %all-to-all-start = ((s32[256,1,1,4,2]{3,4,2,1,0:T(2,128)}), s32[256,1,1,4,2]{3,4,2,1,0:T(2,128)S(1)}, u32[]{:S(2)}, u32[]{:S(2)}) async-start(s32[256,1,1,4,2]{3,4,2,1,0:T(2,128)} %copy.14), calls=%async_computation | async-start | bytes 524288 | tf_op jit(solution)/shard_map/all_to_all | solution.py:50
  64.3 8.6 %scatter_custom_fusion.2 = s32[1024,2048]{1,0:T(8,128)} fusion(s32[512]{0:T(512)S(1)} %get-tuple-element.5, s32[512,2048]{1,0:T(8,128)} %param.7, s32[]{:T(128)} %constant.97.clone.1), kind=kCustom, calls=%fused_computation.8 | custom fusion | bytes 8389120 | tf_op jit(solution)/shard_map/scatter | solution.py:85
  72.9 9.8 %reshape_transpose_transpose_reshape_reshape_reshape.7 = s32[256,1,1,4,2048]{4,3,0,2,1:T(4,128)} reshape(s32[1024,2048]{1,0:T(8,128)} %scatter_custom_fusion.2) | data formatting | bytes 16777216 | tf_op jit(solution)/shard_map/reshape;transpose;transpose;reshape;reshape;reshape | solution.py:49
  82.7 14.9 %all-to-all-start.1 = ((s32[256,1,1,4,2048]{4,3,2,1,0:T(4,128)}), s32[256,1,1,4,2048]{4,3,2,1,0:T(4,128)}, u32[]{:S(2)}, u32[]{:S(2)}) async-start(s32[256,1,1,4,2048]{4,3,2,1,0:T(4,128)} %bitcast.102), calls=%async_computation.1 | async-start | bytes 16777216 | tf_op jit(solution)/shard_map/all_to_all | solution.py:50
  97.6 3.3 scatter_custom_fusion
  100.8 222.9 %psum.7 = f32[4096]{0:T(1024)S(1)} all-reduce(f32[4096]{0:T(1024)S(1)} %scatter_custom_fusion), channel_id=1, replica_groups=mesh['dp_0'=4,'dp_1'=8,'group_0'=4,'group_1'=2] {'dp_0','dp_1','group_0'..., use_global_device_ids=true, to_apply=%region_1.2 | all-reduce | flops 4096 | bytes 32768 | tf_op jit(solution)/shard_map/psum | solution.py:75
  326.6 6.2 %gather_fusion = f32[1024]{0:T(1024)S(1)} fusion(f32[4096]{0:T(1024)S(1)} %rev.7, s32[1024]{0:T(1024)S(1)} %broadcast_clamp_fusion), kind=kCustom, calls=%fused_computation | custom fusion | bytes 12288 | tf_op jit(solution)/shard_map/gather | solution.py:102
  332.8 4.9 %scatter_custom_fusion.4 = f32[1024]{0:T(1024)} fusion(s32[1024]{0:T(1024)S(1)} %bitcast.116, f32[1024]{0:T(1024)S(1)} %divide_select_fusion, f32[]{:T(128)} %constant.95.clone.1), kind=kCustom, calls=%fused_computation.65 | custom fusion | bytes 4100 | tf_op jit(solution)/shard_map/scatter | solution.py:104
  337.7 10.0 %reshape.165 = s32[1024,2048]{1,0:T(8,128)} reshape(s32[32,8,1,4,2048]{4,3,1,0,2:T(4,128)} %bitcast.31) | data formatting | bytes 16777216 | tf_op jit(solution)/shard_map/reshape;reshape | solution.py:94
  347.7 13.0 %scatter_custom_fusion.3 = s32[1024,2048]{1,0:T(8,128)} fusion(s32[1024]{0:T(1024)S(1)} %bitcast.117, s32[1024,2048]{1,0:T(8,128)} %reshape.165, s32[]{:T(128)} %constant.97.clone.1), kind=kCustom, calls=%fused_computation.6 | custom fusion | bytes 8389120 | tf_op jit(solution)/shard_map/scatter | solution.py:103
  (32 shorter events, 3.8 us)
Async XLA Ops:
  51.1 31.6 %all-to-all-start = ((s32[256,1,1,4,2]{3,4,2,1,0:T(2,128)}), s32[256,1,1,4,2]{3,4,2,1,0:T(2,128)S(1)}, u32[]{:S(2)}, u32[]{:S(2)}) async-start(s32[256,1,1,4,2]{3,4,2,1,0:T(2,128)} %copy.14), calls=%async_computation | async-start | bytes 524288 | tf_op jit(solution)/shard_map/all_to_all | solution.py:50
  82.7 255.0 %all-to-all-start.1 = ((s32[256,1,1,4,2048]{4,3,2,1,0:T(4,128)}), s32[256,1,1,4,2048]{4,3,2,1,0:T(4,128)}, u32[]{:S(2)}, u32[]{:S(2)}) async-start(s32[256,1,1,4,2048]{4,3,2,1,0:T(4,128)} %bitcast.102), calls=%async_computation.1 | async-start | bytes 16777216 | tf_op jit(solution)/shard_map/all_to_all | solution.py:50
where the time goes:
time: 362 us; the launch traced here: 361 us
  blocking collectives  258 us (71%)
  local copies, waits for them, and re-layouts  60.7 us (17%)
  starting transfers between devices  28 us (8%)
  other arithmetic  10.4 us (3%)
    psum x1, blocking collectives, body(): hist = lax.psum(local_hist, DP_GROUP)  223 us
    all_to_all x2, starting transfers between devices, exchange_both(): tiles = lax.all_to_all(tiles, axis, split_axis=0, concat_axis=0, tiled=True)  28 us
    all_gather x2, blocking collectives, prefix_by_axis(): pieces = lax.all_gather(so_far, axis)  23.3 us
    scatter x1, local copies, waits for them, and re-layouts, body(): jnp.zeros((capacity, width), jnp.int32).at[target]  13 us
    another operation x2, local copies, waits for them, and re-layouts, exchange_both(): tiles = tiles.reshape(-1, *inside)  12.1 us
    unnamed x2, blocking collectives  12 us
    another operation x1, local copies, waits for them, and re-layouts, body(): got_rows = got_rows.reshape(-1, width)  10 us
    scatter x1, local copies, waits for them, and re-layouts, body(): jnp.zeros((outside, width), jnp.int32).at[position_send]  8.6 us
  transfers between devices with their start and end apart: 2, of which 0 were waited for; matrix products, arithmetic and copies ran while one was open for 10% of the time, Pallas kernels for 0%

commit v1 on v0

--- a/solution.py
+++ b/solution.py
@@ -72,7 +72,7 @@
     ).astype(jnp.int32)
     counts = jnp.sum(onehot, axis=0).astype(jnp.float32)
     before = prefix_by_axis(counts, DP_GROUP, add_counts, jnp.zeros_like(counts))
-    hist = lax.psum(local_hist, DP_GROUP)
+    hist = jnp.sum(lax.all_gather(local_hist, DP_GROUP), axis=0)
     running = jnp.cumsum(onehot, axis=0) - onehot
     local_rank = jnp.sum(running * onehot, axis=1)
     offset = jnp.sum(before.astype(jnp.int32)[None, :] * onehot, axis=1)

time: 362 us -> 332 us (0.917)
  blocking collectives: 258 us -> 35.4 us
  waiting for transfers between devices: 0.01 us -> 172 us
  between operations: 3.41 us -> 16.8 us
  local copies, waits for them, and re-layouts: 60.7 us -> 65.6 us
    psum x1 -> x0, blocking collectives: 223 us -> none  [body(): hist = lax.psum(local_hist, DP_GROUP)]
    all_gather x0 -> x1, waiting for transfers between devices: none -> 137 us  [body(): hist = jnp.sum(lax.all_gather(local_hist, DP_GROUP), axis=0)]
    all_to_all x2, waiting for transfers between devices: 0.01 us -> 34.3 us  [exchange_both(): tiles = lax.all_to_all(tiles, axis, split_axis=0, concat_axis=0, tiled=True)]
    all_gather x0 -> x1, local copies, waits for them, and re-layouts: none -> 4.94 us  [body(): hist = jnp.sum(lax.all_gather(local_hist, DP_GROUP), axis=0)]
  transfers between devices with their start and end apart: 2 -> 3, of which waited for: 0 -> 2; matrix products, arithmetic and copies ran while one was open for 10% -> 13% of each run, Pallas kernels for 0% -> 0%
where the time goes in v1:
time: 332 us; the launch traced here: 331 us
  waiting for transfers between devices  172 us (52%)
  local copies, waits for them, and re-layouts  65.6 us (20%)
  blocking collectives  35.4 us (11%)
  starting transfers between devices  28.1 us (8%)
  between operations  16.8 us (5%)
  other arithmetic  13.3 us (4%)
    all_gather x1, waiting for transfers between devices, body(): hist = jnp.sum(lax.all_gather(local_hist, DP_GROUP), axis=0)  137 us
    all_to_all x2, waiting for transfers between devices, exchange_both(): tiles = lax.all_to_all(tiles, axis, split_axis=0, concat_axis=0, tiled=True)  34.3 us
    all_to_all x2, starting transfers between devices, exchange_both(): tiles = lax.all_to_all(tiles, axis, split_axis=0, concat_axis=0, tiled=True)  28 us
    all_gather x2, blocking collectives, prefix_by_axis(): pieces = lax.all_gather(so_far, axis)  23.3 us
    scatter x1, local copies, waits for them, and re-layouts, body(): jnp.zeros((capacity, width), jnp.int32).at[target]  13 us
    another operation x2, local copies, waits for them, and re-layouts, exchange_both(): tiles = tiles.reshape(-1, *inside)  12.1 us
    unnamed x2, blocking collectives  12 us
    another operation x1, local copies, waits for them, and re-layouts, body(): got_rows = got_rows.reshape(-1, width)  10 us
  transfers between devices with their start and end apart: 3, of which 2 were waited for; matrix products, arithmetic and copies ran while one was open for 13% of the time, Pallas kernels for 0%

profile of v1, /device:TPU:1, one launch (start us, length us, event | category | flops | bytes accessed | tf_op | source)
XLA Modules:
  0.0 330.8 jit_solution(4825490791358095705)
XLA Ops:
  8.5 0.8 convert_reduce_fusion
  9.3 1.3 dynamic-slice
  11.4 5.3 %all-reduce = f32[64]{0:T(128)S(1)} all-reduce(f32[64]{0:T(128)S(1)} %convert_dynamic-update-slice_fusion), channel_id=3, replica_groups=mesh['dp_0'=4,'dp_1'=8,'group_0'=4,'group_1'=2] {'group_1'}, use_global_device_ids=true, to_apply=%add | all-reduce | flops 64 | bytes 512
  16.7 1.3 dynamic-slice.1
  18.8 6.7 %all-reduce.1 = f32[128]{0:T(128)S(1)} all-reduce(f32[128]{0:T(128)S(1)} %fusion.35), channel_id=4, replica_groups=mesh['dp_0'=4,'dp_1'=8,'group_0'=4,'group_1'=2] {'group_0'}, use_global_device_ids=true, to_apply=%add.1 | all-reduce | flops 128 | bytes 1024
  25.6 15.4 %all-gather.3 = f32[8,1,32]{2,1,0:T(1,128)S(1)} all-gather(f32[1,1,32]{2,1,0:T(1,128)S(1)} %fusion.37), channel_id=1, replica_groups=mesh['dp_0'=4,'dp_1'=8,'group_0'=4,'group_1'=2] {'dp_1'}, dimensions={0}, use_global_device_ids=true | all-gather | bytes 1152 | tf_op jit(solution)/shard_map/all_gather | solution.py:23
  41.0 7.9 %all-gather.4 = f32[4,1,32]{2,1,0:T(1,128)S(1)} all-gather(f32[1,1,32]{2,1,0:T(1,128)S(1)} %bitcast.115), channel_id=1, replica_groups=mesh['dp_0'=4,'dp_1'=8,'group_0'=4,'group_1'=2] {'dp_0'}, dimensions={0}, use_global_device_ids=true | all-gather | bytes 640 | tf_op jit(solution)/shard_map/all_gather | solution.py:23
  49.6 1.2 reduce-window.15
  51.1 0.8 select_reduce_fusion
  53.5 1.8 scatter_custom_fusion.1
  55.3 2.3 copy.20
  57.6 13.2 %all-to-all-start = ((s32[256,1,1,4,2]{3,4,2,1,0:T(2,128)}), s32[256,1,1,4,2]{3,4,2,1,0:T(2,128)S(1)}, u32[]{:S(2)}, u32[]{:S(2)}) async-start(s32[256,1,1,4,2]{3,4,2,1,0:T(2,128)} %copy.20), calls=%async_computation | async-start | bytes 524288 | tf_op jit(solution)/shard_map/all_to_all | solution.py:50
  70.8 8.6 %scatter_custom_fusion.2 = s32[1024,2048]{1,0:T(8,128)} fusion(s32[512]{0:T(512)S(1)} %get-tuple-element.5, s32[512,2048]{1,0:T(8,128)} %param.7, s32[]{:T(128)} %constant.97.clone.1), kind=kCustom, calls=%fused_computation.8 | custom fusion | bytes 8389120 | tf_op jit(solution)/shard_map/scatter | solution.py:85
  79.4 9.8 %reshape_transpose_transpose_reshape_reshape_reshape.7 = s32[256,1,1,4,2048]{4,3,0,2,1:T(4,128)} reshape(s32[1024,2048]{1,0:T(8,128)} %scatter_custom_fusion.2) | data formatting | bytes 16777216 | tf_op jit(solution)/shard_map/reshape;transpose;transpose;reshape;reshape;reshape | solution.py:49
  89.2 14.9 %all-to-all-start.1 = ((s32[256,1,1,4,2048]{4,3,2,1,0:T(4,128)}), s32[256,1,1,4,2048]{4,3,2,1,0:T(4,128)}, u32[]{:S(2)}, u32[]{:S(2)}) async-start(s32[256,1,1,4,2048]{4,3,2,1,0:T(4,128)} %bitcast.102), calls=%async_computation.1 | async-start | bytes 16777216 | tf_op jit(solution)/shard_map/all_to_all | solution.py:50
  104.1 3.8 %scatter_custom_fusion = f32[4096]{0:T(1024)} fusion(s32[512]{0:T(512)S(1)} %compare_select_fusion.7, f32[512]{0:T(512)S(1)} %broadcast.158, f32[]{:T(128)} %constant.95.clone.1), kind=kCustom, calls=%fused_computation.36 | custom fusion | flops 512 | bytes 16388 | tf_op jit(solution)/shard_map/scatter-add | solution.py:67
  108.3 137.4 %all-gather.7.cloned.1.call-done = f32[1048576]{0:T(1024)} async-done(((f32[4096]{0:T(1024)}), f32[1048576]{0:T(1024)}) %all-gather.7.cloned.1.call-update) | async-done | bytes 4194320 | tf_op jit(solution)/shard_map/all_gather | solution.py:75
  245.7 4.9 %reshape.177 = f32[256,4096]{1,0:T(8,128)} reshape(f32[1048576]{0:T(1024)} %all-gather.7.cloned.1.call-done) | data formatting | bytes 8388608 | tf_op jit(solution)/shard_map/all_gather | solution.py:75
  250.6 2.4 reduce_sum.36
  254.4 6.2 %gather_fusion = f32[1024]{0:T(1024)S(1)} fusion(f32[4096]{0:T(1024)S(1)} %rev.7, s32[1024]{0:T(1024)S(1)} %broadcast_clamp_fusion), kind=kCustom, calls=%fused_computation | custom fusion | bytes 12288 | tf_op jit(solution)/shard_map/gather | solution.py:102
  261.8 4.9 %scatter_custom_fusion.4 = f32[1024]{0:T(1024)} fusion(s32[1024]{0:T(1024)S(1)} %bitcast.116, f32[1024]{0:T(1024)S(1)} %divide_select_fusion, f32[]{:T(128)} %constant.95.clone.1), kind=kCustom, calls=%fused_computation.65 | custom fusion | bytes 4100 | tf_op jit(solution)/shard_map/scatter | solution.py:104
  266.7 34.3 %all-to-all-done.1 = s32[256,1,1,4,2048]{4,3,2,1,0:T(4,128)} async-done(((s32[256,1,1,4,2048]{4,3,2,1,0:T(4,128)}), s32[256,1,1,4,2048]{4,3,2,1,0:T(4,128)}, u32[]{:S(2)}, u32[]{:S(2)}) %all-to-all-start.1) | async-done | bytes 8388640 | tf_op jit(solution)/shard_map/all_to_all | solution.py:50
  300.9 10.0 %reshape.165 = s32[1024,2048]{1,0:T(8,128)} reshape(s32[32,8,1,4,2048]{4,3,1,0,2:T(4,128)} %bitcast.31) | data formatting | bytes 16777216 | tf_op jit(solution)/shard_map/reshape;reshape | solution.py:94
  311.0 13.0 %scatter_custom_fusion.3 = s32[1024,2048]{1,0:T(8,128)} fusion(s32[1024]{0:T(1024)S(1)} %bitcast.117, s32[1024,2048]{1,0:T(8,128)} %reshape.165, s32[]{:T(128)} %constant.97.clone.1), kind=kCustom, calls=%fused_computation.6 | custom fusion | bytes 8389120 | tf_op jit(solution)/shard_map/scatter | solution.py:103
  (36 shorter events, 5.9 us)
Async XLA Ops:
  57.6 31.6 %all-to-all-start = ((s32[256,1,1,4,2]{3,4,2,1,0:T(2,128)}), s32[256,1,1,4,2]{3,4,2,1,0:T(2,128)S(1)}, u32[]{:S(2)}, u32[]{:S(2)}) async-start(s32[256,1,1,4,2]{3,4,2,1,0:T(2,128)} %copy.20), calls=%async_computation | async-start | bytes 524288 | tf_op jit(solution)/shard_map/all_to_all | solution.py:50
  89.2 211.7 %all-to-all-start.1 = ((s32[256,1,1,4,2048]{4,3,2,1,0:T(4,128)}), s32[256,1,1,4,2048]{4,3,2,1,0:T(4,128)}, u32[]{:S(2)}, u32[]{:S(2)}) async-start(s32[256,1,1,4,2048]{4,3,2,1,0:T(4,128)} %bitcast.102), calls=%async_computation.1 | async-start | bytes 16777216 | tf_op jit(solution)/shard_map/all_to_all | solution.py:50
  104.1 141.6 %all-gather.7.cloned.1.call-start = ((), (), s32[]{:S(2)}) async-start(), calls=%async_computation.2 | async-start | bytes 4210688 | tf_op jit(solution)/shard_map/all_gather | solution.py:75
Sparse Core Ops, SparseCore 0:
  109.0 136.5 all-gather.6
